TPU v7x, 32 devices: a whole 2x2x4 slice. The times are simulated.
32 devices in a mesh: groups: 2 (over x), traces: 16 (over z, y, core).
Axes of the slice: x: 2, y: 2, z: 4, core: 2. Of those that a mesh axis runs over, the one named last changes fastest.
Arguments:
- raw_traces: float32 [8192, 8192], P(('groups', 'traces')), parts along dimension 0, may hold values from -6 to 6
- filter_index: int32 [8192], P(('groups', 'traces')), parts along dimension 0, may hold values from 0 to 255
- channel_order: int32 [512], P('groups'), parts along dimension 0, may hold values from 0 to 255, each once
- wavelets: float32 [256, 256], P('traces'), may hold values from -0.375 to 0.375
- damping: float32 [256], P('traces'), may hold values from 0.02 to 0.5
Outputs:
- deconvolved: float32 [8192, 8192], P(('groups', 'traces')), parts along dimension 0
There are 2 independent parts, one for each index of `groups`. A program takes and returns all parts, laid end to end along the dimension named above; an argument that names none is the same for every part. Nothing has to cross between parts.
Inputs may be any that keep to these rules, and one draw needn't show every extreme that they name: `channel_order`: each of 0 to 255 appears once.
All inputs are finite; a program needn't handle non-finite values.
Results may differ from a plain program's by a relative error of at most 0.00021.
Values sent between devices are 32-bit elements; how exact they have to be, the bound alone decides.
A program may use at most 192 MiB of HBM per device.

v0:
```python
import math

import jax
import jax.numpy as jnp
from jax import lax
from jax.sharding import PartitionSpec as P

P_SIZE = 64


HIGHEST = lax.Precision.HIGHEST


def angle_table(height, across, period, orient):
    row_ids = lax.broadcasted_iota(jnp.int32, (height, across), 0)
    col_ids = lax.broadcasted_iota(jnp.int32, (height, across), 1)
    phases = (row_ids * col_ids % period).astype(jnp.float32) * (2.0 * math.pi / period)
    return (jnp.cos(phases), orient * jnp.sin(phases))


def forward_spectra(signal, factor):
    traces_here, length = signal.shape
    second = length // factor
    blocks = signal.reshape(traces_here, factor, second)
    cos_p, sin_p = angle_table(factor, factor, factor, -1.0)
    first_re = jnp.einsum("tnq,nk->tkq", blocks, cos_p, precision=HIGHEST)
    first_im = jnp.einsum("tnq,nk->tkq", blocks, sin_p, precision=HIGHEST)
    twist_c, twist_s = angle_table(factor, second, length, -1.0)
    mid_re = first_re * twist_c - first_im * twist_s
    mid_im = first_re * twist_s + first_im * twist_c
    cos_q, sin_q = angle_table(second, second, second, -1.0)
    out_re = jnp.einsum("tkq,qm->tkm", mid_re, cos_q, precision=HIGHEST) - jnp.einsum(
        "tkq,qm->tkm", mid_im, sin_q, precision=HIGHEST
    )
    out_im = jnp.einsum("tkq,qm->tkm", mid_re, sin_q, precision=HIGHEST) + jnp.einsum(
        "tkq,qm->tkm", mid_im, cos_q, precision=HIGHEST
    )
    return (out_re, out_im)


def inverse_signal(spec_re, spec_im):
    traces_here, factor, second = spec_re.shape
    length = factor * second
    cos_q, sin_q = angle_table(second, second, second, 1.0)
    back_re = jnp.einsum("tkm,mq->tkq", spec_re, cos_q, precision=HIGHEST) - jnp.einsum(
        "tkm,mq->tkq", spec_im, sin_q, precision=HIGHEST
    )
    back_im = jnp.einsum("tkm,mq->tkq", spec_re, sin_q, precision=HIGHEST) + jnp.einsum(
        "tkm,mq->tkq", spec_im, cos_q, precision=HIGHEST
    )
    twist_c, twist_s = angle_table(factor, second, length, 1.0)
    turned_re = back_re * twist_c - back_im * twist_s
    turned_im = back_re * twist_s + back_im * twist_c
    cos_p, sin_p = angle_table(factor, factor, factor, 1.0)
    signal = jnp.einsum("tkq,kn->tnq", turned_re, cos_p, precision=HIGHEST) - jnp.einsum(
        "tkq,kn->tnq", turned_im, sin_p, precision=HIGHEST
    )
    return (signal / length).reshape(traces_here, length)


def gains_from(wavelets, damping, length):
    padded = jnp.pad(wavelets, ((0, 0), (0, length - wavelets.shape[1])))
    spec_re, spec_im = forward_spectra(padded, P_SIZE)
    power = spec_re * spec_re + spec_im * spec_im
    level = jnp.mean(power, axis=(1, 2), keepdims=True)
    denom = power + damping[:, None, None] * (level + 1e-06)
    return (spec_re / denom, -spec_im / denom)


def local(raw_traces, filter_index, channel_order, wavelets, damping):
    length = raw_traces.shape[1]
    own_re, own_im = gains_from(wavelets, damping, length)
    gain_re, gain_im = (
        lax.all_gather(own_re, "traces", axis=0, tiled=True),
        lax.all_gather(own_im, "traces", axis=0, tiled=True),
    )
    spec_re, spec_im = forward_spectra(raw_traces, P_SIZE)
    pick_re = jnp.take(gain_re, filter_index, axis=0)
    pick_im = jnp.take(gain_im, filter_index, axis=0)
    out_re = spec_re * pick_re - spec_im * pick_im
    out_im = spec_re * pick_im + spec_im * pick_re
    result = inverse_signal(out_re, out_im)
    groups_n = lax.axis_size("traces")
    rows_here = result.shape[0]
    stacked = result.reshape(groups_n, rows_here // groups_n, 1, length)
    moved = lax.all_to_all(stacked, "traces", split_axis=0, concat_axis=2, tiled=True)
    ordered = moved.reshape(rows_here, length)
    return jnp.take(ordered, channel_order, axis=0)


def solution(mesh):
    placed = (
        P(("groups", "traces"), None),
        P(("groups", "traces")),
        P("groups"),
        P("traces", None),
        P("traces"),
    )
    return jax.shard_map(
        local, mesh=mesh, in_specs=placed, out_specs=P(("groups", "traces"), None), check_vma=False
    )
```

profile of v0, /device:TPU:13, one launch (start us, length us, event | category | flops | bytes accessed | tf_op | source)
XLA Modules:
  0.0 531.2 jit_solution(3008212875347304327)
XLA Ops:
  6.5 0.0 all-gather.5.cloned.1.call-start
  6.5 0.1 broadcast_multiply_fusion
  6.7 0.8 pad_bitcast_fusion
  7.4 0.1 copy.33
  7.6 0.7 fusion.54
  8.3 0.7 fusion.59
  9.0 0.8 fusion.16
  9.9 0.8 fusion.18
  10.7 0.8 convolution_subtract_fusion
  11.5 0.9 fusion.20
  12.5 0.0 copy-done.5
  12.5 1.2 negate_divide_fusion
  13.6 0.0 all-gather.5.cloned.1.call-update
  13.7 0.3 all-gather.3.cloned.1.call-start
  13.9 0.5 all-gather.3.cloned.1.call-update
  14.4 0.0 copy-start.3
  14.4 5.0 copy.32
  19.4 0.0 copy-done.3
  19.5 0.0 copy-start.1
  19.5 0.1 fusion.91
  19.6 3.1 copy-done.1
  22.7 9.8 %fusion.56 = f32[64,256,128]{2,0,1:T(8,128)} fusion(f32[256,64,128]{2,1,0:T(8,128)S(1)} %bitcast.91), kind=kOutput, calls=%fused_computation.84 | convolution fusion | flops 1610674176 | bytes 16777216 | tf_op jit(solution)/shard_map/tnq,nk->tkq/dot_general | solution.py:27
  32.5 13.6 %add_bitcast_fusion = (f32[256,64,128]{2,1,0:T(8,128)S(1)}, f32[256,64,128]{2,1,0:T(8,128)S(1)}) fusion(f32[64,256,128]{2,0,1:T(8,128)} %fusion.56, f32[64,128]{1,0:T(8,128)S(1)} %get-tuple-element.16, f32[64,128]{1,0:T(8,128)S(1)} %get-tuple-element.17, f32[256,64,128]{2,1,0:T(8,128)} %bitcast.92), kind=kOutput, calls=%fused_computation.14 | convolution fusion | flops 1623252992 | bytes 33619968 | tf_op jit(solution)/shard_map/tnq,nk->tkq/dot_general | solution.py:26
  46.1 0.0 copy-start
  46.1 15.8 %fusion.4 = f32[256,64,128]{2,0,1:T(8,128)} fusion(f32[256,64,128]{2,1,0:T(8,128)S(1)} %get-tuple-element.10), kind=kOutput, calls=%fused_computation.16 | convolution fusion | flops 3221454848 | bytes 16777216 | tf_op jit(solution)/shard_map/tkq,qm->tkm/dot_general | solution.py:35
  62.0 16.0 %fusion.6 = f32[256,64,128]{2,0,1:T(8,128)} fusion(f32[256,64,128]{2,1,0:T(8,128)S(1)} %get-tuple-element.10), kind=kOutput, calls=%fused_computation.18 | convolution fusion | flops 3221471232 | bytes 16777216 | tf_op jit(solution)/shard_map/tkq,qm->tkm/dot_general | solution.py:32
  78.0 0.0 copy-done
  78.0 15.7 %fusion.10 = f32[256,64,128]{2,0,1:T(8,128)} fusion(f32[256,64,128]{2,1,0:T(8,128)S(1)} %get-tuple-element.11), kind=kOutput, calls=%fused_computation.22 | convolution fusion | flops 3221454848 | bytes 16777216 | tf_op jit(solution)/shard_map/tkq,qm->tkm/dot_general | solution.py:32
  93.7 7.7 %gather_fusion.2 = f32[256,64,128]{2,1,0:T(8,128)} fusion(f32[256,64,128]{2,1,0:T(8,128)} %all-gather.5.cloned.1.call-done, s32[1024]{0:T(1024)S(1)} %pad_clamp_fusion.1), kind=kCustom, calls=%fused_computation.1.clone | custom fusion | bytes 16778240 | tf_op jit(solution)/shard_map/jit(_take)/gather | solution.py:79
  101.4 62.2 %all-gather.3.cloned.1.call-done = f32[256,64,128]{2,1,0:T(8,128)} async-done(((f32[16,64,128]{2,1,0:T(8,128)}), f32[256,64,128]{2,1,0:T(8,128)}) %all-gather.3.cloned.1.call-update) | async-done | bytes 8388624 | tf_op jit(solution)/shard_map/all_gather | solution.py:74
  163.5 7.9 %gather_fusion.1 = f32[256,64,128]{2,1,0:T(8,128)} fusion(f32[256,64,128]{2,1,0:T(8,128)} %all-gather.3.cloned.1.call-done, s32[1024]{0:T(1024)S(1)} %pad_clamp_fusion.1), kind=kCustom, calls=%fused_computation.clone | custom fusion | bytes 16778240 | tf_op jit(solution)/shard_map/jit(_take)/gather | solution.py:78
  171.4 38.6 %multiply_add_fusion.1 = (f32[256,64,128]{2,0,1:T(8,128)}, f32[256,64,128]{2,0,1:T(8,128)}) fusion(f32[256,64,128]{2,1,0:T(8,128)} %gather_fusion.1, f32[256,64,128]{2,1,0:T(8,128)} %gather_fusion.2, pred[256]{0:T(512)(128)(4,1)S(1)} %compare_and_fusion, f32[256,64,128]{2,0,1:T(8,128)} %fusion.4, f32[256,64,128]{2,0,1:T(8,128)} %fusion.10, ...), kind=kOutput, calls=%fused_computation.12 | convolution fusion | flops 3242442752 | bytes 67109120 | tf_op jit(solution)/shard_map/tkq,qm->tkm/dot_general | solution.py:35
  210.0 0.0 slice-start.2
  210.0 12.7 %fusion.32 = f32[256,64,128]{2,0,1:T(8,128)} fusion(f32[256,64,128]{2,0,1:T(8,128)} %get-tuple-element.6), kind=kOutput, calls=%fused_computation.54 | convolution fusion | flops 3221454848 | bytes 16777216 | tf_op jit(solution)/shard_map/tkm,mq->tkq/dot_general | solution.py:48
  222.7 0.0 slice-done
  222.7 0.0 slice-done.1
  222.7 9.3 %fusion.26 = f32[256,64,128]{2,0,1:T(8,128)} fusion(f32[256,64,128]{2,0,1:T(8,128)S(1)} %bitcast.88), kind=kOutput, calls=%fused_computation.48 | convolution fusion | flops 3221454848 | bytes 16777216 | tf_op jit(solution)/shard_map/tkm,mq->tkq/dot_general | solution.py:45
  232.0 0.0 slice-done.3
  232.0 9.3 %fusion.34 = f32[256,64,128]{2,0,1:T(8,128)} fusion(f32[256,64,128]{2,0,1:T(8,128)S(1)} %bitcast.90), kind=kOutput, calls=%fused_computation.56 | convolution fusion | flops 3221454848 | bytes 16777216 | tf_op jit(solution)/shard_map/tkm,mq->tkq/dot_general | solution.py:45
  241.4 18.5 %multiply_subtract_fusion = (f32[256,64,128]{2,0,1:T(8,128)}, f32[256,64,128]{2,0,1:T(8,128)}) fusion(f32[64,128]{1,0:T(8,128)S(1)} %fusion.91, f32[64,128]{1,0:T(8,128)S(1)} %get-tuple-element.17, f32[256,64,128]{2,0,1:T(8,128)} %fusion.32, f32[256,64,128]{2,0,1:T(8,128)} %fusion.34, f32[256,64,128]{2,0,1:T(8,128)} %fusion.26, ...), kind=kOutput, calls=%fused_computation.11 | convolution fusion | flops 3238232064 | bytes 50397184 | tf_op jit(solution)/shard_map/tkm,mq->tkq/dot_general | solution.py:48
  259.9 15.6 %fusion = f32[64,256,128]{2,0,1:T(8,128)S(1)} fusion(f32[256,64,128]{2,0,1:T(8,128)} %get-tuple-element.9), kind=kOutput, calls=%fused_computation.3 | convolution fusion | flops 1610670080 | bytes 16777216 | tf_op jit(solution)/shard_map/tkq,kn->tnq/dot_general | solution.py:55
  275.6 17.5 %multiply_bitcast_fusion = f32[256,64,128]{2,1,0:T(8,128)} fusion(f32[64,256,128]{2,0,1:T(8,128)S(1)} %fusion, f32[256,64,128]{2,0,1:T(8,128)S(1)} %copy-done.2), kind=kOutput, calls=%fused_computation.9 | convolution fusion | flops 1614864384 | bytes 25165824 | tf_op jit(solution)/shard_map/tkq,kn->tnq/dot_general | solution.py:55
  293.1 9.4 %reshape_reshape.3 = f32[16,16,1,8192]{3,1,0,2:T(8,128)} reshape(f32[256,64,128]{2,1,0:T(8,128)} %multiply_bitcast_fusion) | data formatting | bytes 16777216 | tf_op jit(solution)/shard_map/reshape;reshape | solution.py:85
  302.5 6.5 %all-to-all-start = ((f32[16,16,1,8192]{3,1,2,0:T(8,128)}), f32[16,16,1,8192]{3,1,2,0:T(8,128)}, u32[]{:S(2)}, u32[]{:S(2)}) async-start(f32[16,16,1,8192]{3,1,2,0:T(8,128)} %bitcast.93), calls=%async_computation | async-start | bytes 16777216 | tf_op jit(solution)/shard_map/all_to_all | solution.py:86
  309.0 182.1 %all-to-all-done = f32[16,16,1,8192]{3,1,2,0:T(8,128)} async-done(((f32[16,16,1,8192]{3,1,2,0:T(8,128)}), f32[16,16,1,8192]{3,1,2,0:T(8,128)}, u32[]{:S(2)}, u32[]{:S(2)}) %all-to-all-start) | async-done | bytes 8388640 | tf_op jit(solution)/shard_map/all_to_all | solution.py:86
  491.1 11.6 %copy.31 = f32[1,16,16,1,8192]{4,2,1,3,0:T(8,128)} copy(f32[1,16,16,1,8192]{4,1,2,3,0:T(8,128)} %bitcast.13) | data formatting | bytes 16777216 | tf_op jit(solution)/shard_map/all_to_all | solution.py:86
  502.7 13.2 %gather_fusion = f32[256,8192]{1,0:T(8,128)} fusion(f32[256,8192]{1,0:T(8,128)} %bitcast.86, s32[1024]{0:T(1024)S(1)} %pad_clamp_fusion), kind=kCustom, calls=%fused_computation.2 | custom fusion | bytes 16778240 | tf_op jit(solution)/shard_map/jit(_take)/gather | solution.py:88
  515.9 8.0 %broadcast_select_fusion = f32[256,8192]{1,0:T(8,128)} fusion(f32[256,8192]{1,0:T(8,128)} %gather_fusion, pred[256]{0:T(512)(128)(4,1)S(1)} %compare_and_fusion.1), kind=kLoop, calls=%fused_computation.24 | loop fusion | flops 2097152 | bytes 16777472 | tf_op jit(solution)/shard_map/jit(_take)/select_n | solution.py:88
  (19 shorter events, 0.1 us)
Async XLA Ops:
  6.5 5.9 %copy-start.5 = (f32[16]{0:T(128)S(1)}, f32[16]{0:T(128)}, u32[]{:S(2)}) copy-start(f32[16]{0:T(128)} %param.11) | copy-start | bytes 196
  6.5 87.1 %all-gather.5.cloned.1.call-start = ((), (), s32[]{:S(2)}) async-start(), calls=%async_computation.2 | async-start | bytes 8912896 | tf_op jit(solution)/shard_map/all_gather | solution.py:75
  13.7 149.9 %all-gather.3.cloned.1.call-start = ((), (), s32[]{:S(2)}) async-start(), calls=%async_computation.1 | async-start | bytes 8912896 | tf_op jit(solution)/shard_map/all_gather | solution.py:74
  14.4 5.0 copy-start.3
  19.5 3.3 copy-start.1
  46.1 31.9 %copy-start = (f32[256,64,128]{2,1,0:T(8,128)}, f32[256,64,128]{2,1,0:T(8,128)S(1)}, u32[]{:S(2)}) copy-start(f32[256,64,128]{2,1,0:T(8,128)S(1)} %get-tuple-element.11) | copy-start | bytes 25165828
  210.0 12.7 %slice-start = ((s8[8388608]{0:T(1024)(128)(4,1)}), s8[4194304]{0:T(1024)(128)(4,1)S(1)}, s32[]{:S(2)}) async-start(s8[8388608]{0:T(1024)(128)(4,1)} %bitcast.87), calls=%async_computation.3 | async-start | bytes 8388608
  210.0 12.7 %slice-start.1 = ((s8[8388608]{0:T(1024)(128)(4,1)}), s8[4194304]{0:T(1024)(128)(4,1)S(1)}, s32[]{:S(2)}) async-start(s8[8388608]{0:T(1024)(128)(4,1)} %bitcast.87), calls=%async_computation.4 | async-start | bytes 8388608
  210.0 22.0 %slice-start.2 = ((s8[8388608]{0:T(1024)(128)(4,1)}), s8[4194304]{0:T(1024)(128)(4,1)S(1)}, s32[]{:S(2)}) async-start(s8[8388608]{0:T(1024)(128)(4,1)} %bitcast.89), calls=%async_computation.5 | async-start | bytes 8388608
  222.7 9.3 %slice-start.3 = ((s8[8388608]{0:T(1024)(128)(4,1)}), s8[4194304]{0:T(1024)(128)(4,1)S(1)}, s32[]{:S(2)}) async-start(s8[8388608]{0:T(1024)(128)(4,1)} %bitcast.89), calls=%async_computation.6 | async-start | bytes 8388608
  259.9 15.6 %copy-start.2 = (f32[256,64,128]{2,0,1:T(8,128)S(1)}, f32[256,64,128]{2,0,1:T(8,128)}, u32[]{:S(2)}) copy-start(f32[256,64,128]{2,0,1:T(8,128)} %get-tuple-element.8) | copy-start | bytes 25165828
  302.5 6.5 %copy-start.4 = (s32[256]{0:T(256)S(1)}, s32[256]{0:T(256)}, u32[]{:S(2)}) copy-start(s32[256]{0:T(256)} %param.9) | copy-start | bytes 3076
  302.5 188.6 %all-to-all-start = ((f32[16,16,1,8192]{3,1,2,0:T(8,128)}), f32[16,16,1,8192]{3,1,2,0:T(8,128)}, u32[]{:S(2)}, u32[]{:S(2)}) async-start(f32[16,16,1,8192]{3,1,2,0:T(8,128)} %bitcast.93), calls=%async_computation | async-start | bytes 16777216 | tf_op jit(solution)/shard_map/all_to_all | solution.py:86
Sparse Core Ops, SparseCore 0:
  13.8 74.6 all-gather.4
  90.6 72.8 all-gather.2
where the time goes:
time: 536 us; the launch traced here: 531 us
  waiting for transfers between devices  245 us (46%)
  matrix products  197 us (37%)
  local copies, waits for them, and re-layouts  58.8 us (11%)
  between operations  14 us (3%)
  other arithmetic  9.46 us (2%)
  starting transfers between devices  6.71 us (1%)
    all_to_all x1, waiting for transfers between devices, local(): lax.all_to_all(stacked, 'traces', split_axis=0, concat_axis=2, tiled=True)  182 us
    all_gather x1, waiting for transfers between devices, local(): lax.all_gather(own_re, 'traces', axis=0, tiled=True)  62.2 us
    dot_general x2, matrix products, forward_spectra(): jnp.einsum('tkq,qm->tkm', mid_re, sin_q, precision=HIGHEST)  39.5 us
    dot_general x1, matrix products, inverse_signal(): jnp.einsum('tkm,mq->tkq', spec_re, sin_q, precision=HIGHEST)  18.5 us
    dot_general x1, matrix products, inverse_signal(): jnp.einsum('tkq,kn->tnq', turned_re, cos_p, precision=HIGHEST)  17.5 us
    dot_general x2, matrix products, forward_spectra(): jnp.einsum('tkq,qm->tkm', mid_im, sin_q, precision=HIGHEST)  16.8 us
    dot_general x2, matrix products, forward_spectra(): jnp.einsum('tkq,qm->tkm', mid_im, cos_q, precision=HIGHEST)  16.8 us
    dot_general x2, matrix products, forward_spectra(): jnp.einsum('tkq,qm->tkm', mid_re, cos_q, precision=HIGHEST)  16.5 us
  transfers between devices with their start and end apart: 3, of which 2 were waited for; matrix products, arithmetic and copies ran while one was open for 16% of the time, Pallas kernels for 0%

commit v1 on v0

v1 whole, which is shorter than its diff:
```python
import functools
import math

import jax
import jax.numpy as jnp
import numpy as np
from jax import lax
from jax.experimental import pallas as pl
from jax.experimental.pallas import tpu as pltpu
from jax.sharding import PartitionSpec as P

LANES = 128
RADIX = 8
ROWS = 16

KEPT = (
    [RADIX * b for b in range(RADIX // 2 + 1)]
    + [a + RADIX * b for a in range(1, RADIX // 2) for b in range(RADIX)]
    + [RADIX // 2 + RADIX * b for b in range(RADIX // 2)]
)
SLOT = {k: s for s, k in enumerate(KEPT)}
KEEP = len(KEPT)


def split_np(table):
    high = jnp.asarray(table, jnp.float32).astype(jnp.bfloat16)
    low = (jnp.asarray(table, jnp.float32) - high.astype(jnp.float32)).astype(jnp.bfloat16)
    return high, low


def lane_matrix(sign, scale):
    ids = np.arange(LANES)
    angle = 2.0 * np.pi * (np.outer(ids, ids) % LANES) / LANES
    c, s = np.cos(angle) * scale, sign * np.sin(angle) * scale
    full = np.block([[c, s], [-s, c]])
    import ml_dtypes

    high = full.astype(np.float32).astype(ml_dtypes.bfloat16)
    low = (full.astype(np.float32) - high.astype(np.float32)).astype(ml_dtypes.bfloat16)
    return np.concatenate([high, high, low], axis=0)


def twiddles(length, taps):
    m = np.arange(LANES)
    rows = []
    for k in KEPT:
        angle = 2.0 * np.pi * k * m / length
        row = [np.cos(angle), -np.sin(angle)]
        weight = 1.0 if k in (0, RADIX * RADIX // 2) else 2.0
        row += [weight * np.cos(angle), weight * np.sin(angle)]
        for piece in range(taps // LANES):
            shifted = 2.0 * np.pi * k * (m + LANES * piece) / length
            row += [np.cos(shifted), -np.sin(shifted)]
        rows.append(np.stack(row))
    return np.stack(rows).astype(np.float32)


def cadd(a, b):
    return (a[0] + b[0], a[1] + b[1])


def csub(a, b):
    return (a[0] - b[0], a[1] - b[1])


def turn(a, num, den):
    num %= den
    if num == 0:
        return a
    if 4 * num == den:
        return (-a[1], a[0])
    if 2 * num == den:
        return (-a[0], -a[1])
    if 4 * num == 3 * den:
        return (a[1], -a[0])
    c, s = math.cos(2 * math.pi * num / den), math.sin(2 * math.pi * num / den)
    return (a[0] * c - a[1] * s, a[0] * s + a[1] * c)


def fourier(items, sign):
    n = len(items)
    if n == 1:
        return items
    even, odd = fourier(items[0::2], sign), fourier(items[1::2], sign)
    turned = [turn(o, sign * k, n) for k, o in enumerate(odd)]
    return [cadd(e, t) for e, t in zip(even, turned)] + [csub(e, t) for e, t in zip(even, turned)]


def real_eight(v):
    h = math.sqrt(0.5)
    s0, d0, s1, d1 = v[0] + v[4], v[0] - v[4], v[1] + v[5], v[1] - v[5]
    s2, d2, s3, d3 = v[2] + v[6], v[2] - v[6], v[3] + v[7], v[3] - v[7]
    p, q = s0 + s2, s1 + s3
    r, t = (d1 - d3) * h, (d1 + d3) * h
    return [p + q, (d0 + r, -(d2 + t)), (s0 - s2, s3 - s1), (d0 - r, d2 - t), p - q]


def eight_real(u0, u1, u2, u3, u4):
    h = math.sqrt(0.5)
    p, q = u0 + u4, u0 - u4
    e = [p + u2[0], q - u2[1], p - u2[0], q + u2[1]]
    f, g = u1[0] - u3[0], u1[1] + u3[1]
    o = [u1[0] + u3[0], (f - g) * h, u3[1] - u1[1], -(f + g) * h]
    return [a + b for a, b in zip(e, o)] + [a - b for a, b in zip(e, o)]


def put_split(ref, base, re, im):
    rows = pl.ds(base, ROWS)
    for part, value in enumerate((re, im)):
        high = value.astype(jnp.bfloat16)
        low = (value - high.astype(jnp.float32)).astype(jnp.bfloat16)
        at = part * LANES
        ref[rows, at : at + LANES] = high
        ref[rows, 2 * LANES + at : 2 * LANES + at + LANES] = low
        ref[rows, 4 * LANES + at : 4 * LANES + at + LANES] = high


def deconvolve(read, write, wave, floor, fwd_ref, inv_ref, tw_ref, mid_ref, cut_ref, spec_ref):
    half, wide = RADIX // 2, RADIX * RADIX
    for j2 in range(RADIX):
        out = real_eight([read(RADIX * j1 + j2) for j1 in range(RADIX)])
        mid_ref[2 * j2] = out[0]
        mid_ref[2 * j2 + 1] = out[half]
        for a in range(1, half):
            mid_ref[2 * RADIX * a + 2 * j2] = out[a][0]
            mid_ref[2 * RADIX * a + 2 * j2 + 1] = out[a][1]

    def emit(k, value):
        s = SLOT[k]
        c, n = tw_ref[s, 0:1, :], tw_ref[s, 1:2, :]
        put_split(cut_ref, s * ROWS, value[0] * c - value[1] * n, value[0] * n + value[1] * c)

    zero = real_eight([mid_ref[2 * j2] for j2 in range(RADIX)])
    c, n = tw_ref[0, 0:1, :], tw_ref[0, 1:2, :]
    for b in range(half + 1):
        s = SLOT[RADIX * b]
        c, n = tw_ref[s, 0:1, :], tw_ref[s, 1:2, :]
        if b in (0, half):
            put_split(cut_ref, s * ROWS, zero[b] * c, zero[b] * n)
        else:
            emit(RADIX * b, zero[b])
    for a in range(1, half):
        base = 2 * RADIX * a
        items = [turn((mid_ref[base + 2 * j2], mid_ref[base + 2 * j2 + 1]), -a * j2, wide) for j2 in range(RADIX)]
        for b, value in enumerate(fourier(items, -1)):
            emit(a + RADIX * b, value)
    four = [mid_ref[2 * j2 + 1] for j2 in range(RADIX)]
    for b in range(half):
        k = half + RADIX * b
        re, im = four[0], None
        for j2 in range(1, RADIX):
            angle = 2 * math.pi * (k * j2 % wide) / wide
            re = re + four[j2] * math.cos(angle)
            term = four[j2] * -math.sin(angle)
            im = term if im is None else im + term
        emit(k, (re, im))

    for s in range(KEEP):
        re = im = None
        for piece, taps in enumerate(wave):
            c, n = tw_ref[s, 4 + 2 * piece : 5 + 2 * piece, :], tw_ref[s, 5 + 2 * piece : 6 + 2 * piece, :]
            re = taps * c if re is None else re + taps * c
            im = taps * n if im is None else im + taps * n
        put_split(cut_ref, (KEEP + s) * ROWS, re, im)

    spec_ref[...] = jnp.dot(cut_ref[...], fwd_ref[...], preferred_element_type=jnp.float32)

    def apply(s, carry):
        at = pl.multiple_of(s * ROWS, ROWS)
        other = pl.multiple_of((KEEP + s) * ROWS, ROWS)
        xr, xi = spec_ref[pl.ds(at, ROWS), 0:LANES], spec_ref[pl.ds(at, ROWS), LANES:]
        hr, hi = spec_ref[pl.ds(other, ROWS), 0:LANES], spec_ref[pl.ds(other, ROWS), LANES:]
        scale = 1.0 / (hr * hr + hi * hi + floor)
        put_split(cut_ref, at, (xr * hr + xi * hi) * scale, (xi * hr - xr * hi) * scale)
        return carry

    lax.fori_loop(0, KEEP, apply, 0, unroll=3)
    rows = KEEP * ROWS
    spec_ref[0:rows] = jnp.dot(cut_ref[0:rows], inv_ref[...], preferred_element_type=jnp.float32)

    def fetch(k):
        s = SLOT[k]
        re, im = spec_ref[s * ROWS : (s + 1) * ROWS, 0:LANES], spec_ref[s * ROWS : (s + 1) * ROWS, LANES:]
        c, n = tw_ref[s, 2:3, :], tw_ref[s, 3:4, :]
        if k in (0, wide // 2):
            return re * c - im * n
        return (re * c - im * n, re * n + im * c)

    for a in range(1, half):
        base = 2 * RADIX * a
        for j2, value in enumerate(fourier([fetch(a + RADIX * b) for b in range(RADIX)], 1)):
            value = turn(value, a * j2, wide)
            mid_ref[base + 2 * j2] = value[0]
            mid_ref[base + 2 * j2 + 1] = value[1]
    for j2, value in enumerate(eight_real(*[fetch(RADIX * b) for b in range(half + 1)])):
        mid_ref[2 * j2] = value
    four = [fetch(half + RADIX * b) for b in range(half)]
    for j2 in range(RADIX):
        total = None
        for b, value in enumerate(four):
            angle = 2 * math.pi * ((half + RADIX * b) * j2 % wide) / wide
            term = value[0] * math.cos(angle)
            if j2:
                term = term - value[1] * math.sin(angle)
            total = term if total is None else total + term
        mid_ref[2 * j2 + 1] = total
    for j2 in range(RADIX):
        parts = [mid_ref[2 * j2]]
        for a in range(1, half):
            base = 2 * RADIX * a
            parts.append((mid_ref[base + 2 * j2], mid_ref[base + 2 * j2 + 1]))
        parts.append(mid_ref[2 * j2 + 1])
        for j1, value in enumerate(eight_real(*parts)):
            write(RADIX * j1 + j2, value)


def block_kernel(taps, x_ref, w_ref, fwd_ref, inv_ref, tw_ref, o_ref, mid_ref, cut_ref, spec_ref):
    def read(j):
        return x_ref[:, j * LANES : (j + 1) * LANES]

    def write(j, value):
        o_ref[:, j * LANES : (j + 1) * LANES] = value

    wave = [w_ref[:, p * LANES : (p + 1) * LANES] for p in range(taps // LANES)]
    deconvolve(read, write, wave, w_ref[:, taps : taps + LANES], fwd_ref, inv_ref, tw_ref, mid_ref, cut_ref, spec_ref)


def tables(length, taps):
    return (
        jnp.asarray(lane_matrix(-1.0, 1.0)),
        jnp.asarray(lane_matrix(1.0, 1.0 / length)),
        jnp.asarray(twiddles(length, taps)),
    )


def scratch():
    return [
        pltpu.VMEM((RADIX * RADIX, ROWS, LANES), jnp.float32),
        pltpu.VMEM((2 * KEEP * ROWS, 6 * LANES), jnp.bfloat16),
        pltpu.VMEM((2 * KEEP * ROWS, 2 * LANES), jnp.float32),
    ]


def local(raw_traces, filter_index, channel_order, wavelets, damping):
    rows, length = raw_traces.shape
    taps = wavelets.shape[1]
    n = lax.axis_size("traces")
    each = rows // n
    floor = damping * (jnp.sum(wavelets * wavelets, axis=1) + 1e-6)
    packed = jnp.concatenate([wavelets, jnp.broadcast_to(floor[:, None], (floor.shape[0], LANES))], axis=1)
    bank = lax.all_gather(packed, "traces", axis=0, tiled=True)
    came = lax.all_to_all(raw_traces.reshape(n, each, length), "traces", 0, 0, tiled=True).reshape(rows, length)
    picks = lax.all_to_all(filter_index.reshape(n, each), "traces", 0, 0, tiled=True).reshape(rows)
    chosen = jnp.take(bank, picks, axis=0)
    fwd, inv, tw = tables(length, taps)
    whole = lambda a: pl.BlockSpec(a.shape, lambda i: (0,) * a.ndim)
    result = pl.pallas_call(
        functools.partial(block_kernel, taps),
        grid=(rows // ROWS,),
        out_shape=jax.ShapeDtypeStruct((rows, length), jnp.float32),
        in_specs=[
            pl.BlockSpec((ROWS, length), lambda i: (i, 0)),
            pl.BlockSpec((ROWS, taps + LANES), lambda i: (i, 0)),
            whole(fwd),
            whole(inv),
            whole(tw),
        ],
        out_specs=pl.BlockSpec((ROWS, length), lambda i: (i, 0)),
        scratch_shapes=scratch(),
        compiler_params=pltpu.CompilerParams(vmem_limit_bytes=40 * 1024 * 1024),
    )(came, chosen, fwd, inv, tw)
    source = (channel_order % n) * each + channel_order // n
    return jnp.take(result, source, axis=0)


def solution(mesh):
    placed = (
        P(("groups", "traces"), None),
        P(("groups", "traces")),
        P("groups"),
        P("traces", None),
        P("traces"),
    )
    return jax.shard_map(
        local, mesh=mesh, in_specs=placed, out_specs=P(("groups", "traces"), None), check_vma=False
    )
```

time: 536 us -> 273 us (0.51)
  waiting for transfers between devices: 245 us -> 0.01 us
  blocking collectives: 0 us -> 203 us
  matrix products: 197 us -> 0 us
  local copies, waits for them, and re-layouts: 58.8 us -> 19.1 us
  Pallas kernels: 0 us -> 32.9 us
  between operations: 14 us -> 0.13 us
    dot_general x18 -> x0, matrix products: 197 us -> none  [the longest x2 39.5 us: forward_spectra(): jnp.einsum('tkq,qm->tkm', mid_re, sin_q, precision=HIGHEST)]
    all_gather x0 -> x1, blocking collectives: none -> 193 us  [local(): bank = lax.all_gather(packed, 'traces', axis=0, tiled=True)]
    all_to_all x1, waiting for transfers between devices: 182 us -> 0.01 us  [local(): lax.all_to_all(raw_traces.reshape(n, each, length), 'traces', 0, 0, tiled...]
    all_gather x2 -> x0, waiting for transfers between devices: 62.2 us -> none  [the longest x1 62.2 us: local(): lax.all_gather(own_re, 'traces', axis=0, tiled=True)]
    pallas_call x0 -> x1, Pallas kernels: none -> 32.9 us  [local(): pl.pallas_call(functools.partial(block_kernel, taps), grid=(rows // ROWS,...]
    gather x3 -> x2, local copies, waits for them, and re-layouts: 28.8 us -> 14.2 us  [the longest x1 13.2 us: local(): return jnp.take(result, source, axis=0)]
    all_to_all x1 -> x2, local copies, waits for them, and re-layouts: 11.6 us -> 1.28 us  [local(): lax.all_to_all(filter_index.reshape(n, each), 'traces', 0, 0, tiled=True)]
    all_to_all x0 -> x1, blocking collectives: none -> 10.2 us  [local(): lax.all_to_all(filter_index.reshape(n, each), 'traces', 0, 0, tiled=True)]
  transfers between devices with their start and end apart: 3 -> 1, of which waited for: 2 -> 0; matrix products, arithmetic and copies ran while one was open for 16% -> 1% of each run, Pallas kernels for 0% -> 0%
where the time goes in v1:
time: 273 us; the launch traced here: 271 us
  blocking collectives  203 us (74%)
  Pallas kernels  32.9 us (12%)
  local copies, waits for them, and re-layouts  19.1 us (7%)
  other arithmetic  8.9 us (3%)
  starting transfers between devices  7.33 us (3%)
    all_gather x1, blocking collectives, local(): bank = lax.all_gather(packed, 'traces', axis=0, tiled=True)  193 us
    pallas_call x1, Pallas kernels, local(): pl.pallas_call(functools.partial(block_kernel, taps), grid=(rows // ROWS,...  32.9 us
    gather x1, local copies, waits for them, and re-layouts, local(): return jnp.take(result, source, axis=0)  13.2 us
    all_to_all x1, blocking collectives, local(): lax.all_to_all(filter_index.reshape(n, each), 'traces', 0, 0, tiled=True)  10.2 us
    select_n x1, other arithmetic, local(): return jnp.take(result, source, axis=0)  7.97 us
    all_to_all x1, starting transfers between devices, local(): lax.all_to_all(raw_traces.reshape(n, each, length), 'traces', 0, 0, tiled...  7.33 us
  transfers between devices with their start and end apart: 1, of which 0 were waited for; matrix products, arithmetic and copies ran while one was open for 1% of the time, Pallas kernels for 0%

profile of v1, /device:TPU:13, one launch (start us, length us, event | category | flops | bytes accessed | tf_op | source)
XLA Modules:
  0.0 271.3 jit_solution(8714555035562443999)
XLA Ops:
  0.0 0.8 all_to_all.10
  0.8 10.2 %all_to_all.14 = s32[16,1,16]{2,1,0:T(1,128)S(1)} all-to-all(s32[16,1,16]{2,1,0:T(1,128)S(1)} %all_to_all.10), channel_id=1, replica_groups=mesh['groups'=2,'traces'=16] {'traces'}, dimensions={0} | all-to-all | bytes 2048 | tf_op jit(solution)/shard_map/all_to_all | solution.py:253
  10.9 0.0 copy-start.5
  10.9 0.0 copy-start.4
  11.0 0.0 copy-start.6
  11.0 0.0 copy-start.1
  11.0 0.0 copy-start.2
  11.0 0.0 copy-start.3
  11.0 7.3 %all-to-all-start = ((f32[16,16,8192]{2,1,0:T(8,128)}), f32[16,16,8192]{2,1,0:T(8,128)}, u32[]{:S(2)}, u32[]{:S(2)}) async-start(f32[16,16,8192]{2,1,0:T(8,128)} %bitcast.4), calls=%async_computation | async-start | bytes 16777216 | tf_op jit(solution)/shard_map/all_to_all | solution.py:252
  18.3 0.0 copy-done.5
  18.4 0.0 copy-done.4
  18.4 0.1 multiply_reduce_fusion
  18.5 0.0 copy-done.6
  18.5 0.1 broadcast_in_dim.30
  18.6 192.7 %all_gather.3 = f32[256,384]{1,0:T(8,128)S(1)} all-gather(f32[16,384]{1,0:T(8,128)S(1)} %pad_maximum_fusion), channel_id=1, replica_groups=mesh['groups'=2,'traces'=16] {'traces'}, dimensions={0}, use_global_device_ids=true | all-gather | bytes 417792 | tf_op jit(solution)/shard_map/all_gather | solution.py:251
  211.3 0.1 reshape.60
  211.4 0.5 broadcast.61
  211.9 0.7 reduce.5
  212.5 0.1 reshape.59
  212.6 1.0 gather_fusion
  213.6 0.1 broadcast_select_fusion.1.w_ref
  213.7 0.0 all-to-all-done
  213.8 0.0 copy-done.1
  213.8 0.0 copy-done.2
  213.8 0.0 copy-done.3
  213.8 32.9 %shard_map.82 = f32[256,8192]{1,0:T(8,128)S(1)} custom-call(f32[256,8192]{1,0:T(8,128)} %bitcast.1.x_ref, f32[256,384]{1,0:T(8,128)S(1)} %broadcast_select_fusion.1.w_ref, bf16[768,256]{1,0:T(8,128)(2,1)S(1)} %copy-done.1, bf16[768,256]{1,0:T(8,128)(2,1)S(1)} %copy-done.2, f32[33,8,128]{2,1,0:T(8,128)S(1)} %copy-done.3), custom_call_target="tpu_custom_call" | custom-call | tf_op jit(solution)/shard_map/pallas_call | solution.py:257
  246.7 0.0 copy-start
  246.7 3.4 %copy-done = f32[256,8192]{1,0:T(8,128)} copy-done((f32[256,8192]{1,0:T(8,128)}, f32[256,8192]{1,0:T(8,128)S(1)}, u32[]{:S(2)}) %copy-start) | copy-done | bytes 8388632
  250.1 13.2 %gather_fusion.1 = f32[256,8192]{1,0:T(8,128)} fusion(f32[256,8192]{1,0:T(8,128)} %copy-done, s32[1024]{0:T(1024)S(1)} %pad_clamp_fusion), kind=kCustom, calls=%fused_computation.1 | custom fusion | bytes 16778240 | tf_op jit(solution)/shard_map/jit(_take)/gather | solution.py:273
  263.3 8.0 %broadcast_select_fusion = f32[256,8192]{1,0:T(8,128)} fusion(f32[256,8192]{1,0:T(8,128)} %gather_fusion.1, pred[256]{0:T(512)(128)(4,1)S(1)} %get-tuple-element.5), kind=kLoop, calls=%fused_computation.2 | loop fusion | flops 2097152 | bytes 16777472 | tf_op jit(solution)/shard_map/jit(_take)/select_n | solution.py:273
  (7 shorter events, 0.1 us)
Async XLA Ops:
  10.9 7.4 %copy-start.5 = (s32[256]{0:T(256)S(1)}, s32[256]{0:T(256)}, u32[]{:S(2)}) copy-start(s32[256]{0:T(256)} %param.10) | copy-start | bytes 3076
  10.9 7.4 %copy-start.4 = (f32[16,256]{1,0:T(8,128)S(1)}, f32[16,256]{1,0:T(8,128)}, u32[]{:S(2)}) copy-start(f32[16,256]{1,0:T(8,128)} %param.11) | copy-start | bytes 49156
  11.0 7.5 %copy-start.6 = (f32[16]{0:T(128)S(1)}, f32[16]{0:T(128)}, u32[]{:S(2)}) copy-start(f32[16]{0:T(128)} %param.12) | copy-start | bytes 196
  11.0 202.8 %copy-start.1 = (bf16[768,256]{1,0:T(8,128)(2,1)S(1)}, bf16[768,256]{1,0:T(8,128)(2,1)}, u32[]{:S(2)}) copy-start(bf16[768,256]{1,0:T(8,128)(2,1)} %constant.66.clone.fwd_ref) | copy-start | bytes 1179652
  11.0 202.8 %copy-start.2 = (bf16[768,256]{1,0:T(8,128)(2,1)S(1)}, bf16[768,256]{1,0:T(8,128)(2,1)}, u32[]{:S(2)}) copy-start(bf16[768,256]{1,0:T(8,128)(2,1)} %constant.67.clone.inv_ref) | copy-start | bytes 1179652
  11.0 202.8 %copy-start.3 = (f32[33,8,128]{2,1,0:T(8,128)S(1)}, f32[33,8,128]{2,1,0:T(8,128)}, u32[]{:S(2)}) copy-start(f32[33,8,128]{2,1,0:T(8,128)} %constant.68.clone.tw_ref) | copy-start | bytes 405508
  11.0 202.8 %all-to-all-start = ((f32[16,16,8192]{2,1,0:T(8,128)}), f32[16,16,8192]{2,1,0:T(8,128)}, u32[]{:S(2)}, u32[]{:S(2)}) async-start(f32[16,16,8192]{2,1,0:T(8,128)} %bitcast.4), calls=%async_computation | async-start | bytes 16777216 | tf_op jit(solution)/shard_map/all_to_all | solution.py:252
  246.7 3.4 %copy-start = (f32[256,8192]{1,0:T(8,128)}, f32[256,8192]{1,0:T(8,128)S(1)}, u32[]{:S(2)}) copy-start(f32[256,8192]{1,0:T(8,128)S(1)} %shard_map.82) | copy-start | bytes 25165828

commit v2 on v1

--- a/solution.py
+++ b/solution.py
@@ -12,6 +12,7 @@
 LANES = 128
 RADIX = 8
 ROWS = 16
+SUBLANES = 8
 
 KEPT = (
     [RADIX * b for b in range(RADIX // 2 + 1)]
@@ -20,12 +21,6 @@
 )
 SLOT = {k: s for s, k in enumerate(KEPT)}
 KEEP = len(KEPT)
-
-
-def split_np(table):
-    high = jnp.asarray(table, jnp.float32).astype(jnp.bfloat16)
-    low = (jnp.asarray(table, jnp.float32) - high.astype(jnp.float32)).astype(jnp.bfloat16)
-    return high, low
 
 
 def lane_matrix(sign, scale):
@@ -214,15 +209,89 @@
             write(RADIX * j1 + j2, value)
 
 
-def block_kernel(taps, x_ref, w_ref, fwd_ref, inv_ref, tw_ref, o_ref, mid_ref, cut_ref, spec_ref):
+def slabs(ref, lead):
+    def at(j):
+        return lead + (slice(None), slice(j * LANES, (j + 1) * LANES))
+
     def read(j):
-        return x_ref[:, j * LANES : (j + 1) * LANES]
+        value = ref[at(j)]
+        return value.reshape(ROWS, LANES)
 
     def write(j, value):
-        o_ref[:, j * LANES : (j + 1) * LANES] = value
-
+        ref[at(j)] = value.reshape(ref[at(j)].shape)
+
+    return read, write
+
+
+def block_kernel(taps, lead, x_ref, w_ref, fwd_ref, inv_ref, tw_ref, o_ref, mid_ref, cut_ref, spec_ref):
+    read, _ = slabs(x_ref, lead)
+    _, write = slabs(o_ref, (slice(None),) * (len(o_ref.shape) - 2))
     wave = [w_ref[:, p * LANES : (p + 1) * LANES] for p in range(taps // LANES)]
     deconvolve(read, write, wave, w_ref[:, taps : taps + LANES], fwd_ref, inv_ref, tw_ref, mid_ref, cut_ref, spec_ref)
+
+
+def place_kernel(taps, row_ref, x_ref, w_ref, fwd_ref, inv_ref, tw_ref, o_ref, mid_ref, cut_ref, spec_ref, res_ref, sems):
+    step, steps = pl.program_id(0), pl.num_programs(0)
+    slot = lax.rem(step, 2)
+
+    def rows_of(at, slot, act):
+        for r in range(ROWS):
+            copy = pltpu.make_async_copy(
+                res_ref.at[slot, pl.ds(r, 1)], o_ref.at[pl.ds(row_ref[at * ROWS + r], 1)], sems.at[slot, r]
+            )
+            act(copy)
+
+    @pl.when(step >= 2)
+    def _():
+        rows_of(step - 2, slot, lambda copy: copy.wait())
+
+    read, _ = slabs(x_ref, (slice(None),) * (len(x_ref.shape) - 2))
+
+    def write(j, value):
+        res_ref[slot, :, j * LANES : (j + 1) * LANES] = value
+
+    wave = [w_ref[:, p * LANES : (p + 1) * LANES] for p in range(taps // LANES)]
+    deconvolve(read, write, wave, w_ref[:, taps : taps + LANES], fwd_ref, inv_ref, tw_ref, mid_ref, cut_ref, spec_ref)
+    rows_of(step, slot, lambda copy: copy.start())
+
+    @pl.when(step == steps - 1)
+    def _():
+        @pl.when(step >= 1)
+        def _():
+            rows_of(step - 1, 1 - slot, lambda copy: copy.wait())
+
+        rows_of(step, slot, lambda copy: copy.wait())
+
+
+def settle_kernel(row_ref, came_ref, filled_ref, o_ref, held_ref, in_sems, out_sems):
+    del filled_ref
+    blocks, rows, _ = came_ref.shape
+
+    def take(d):
+        return pltpu.make_async_copy(came_ref.at[d], held_ref.at[d], in_sems.at[d])
+
+    def put(d, r):
+        return pltpu.make_async_copy(
+            held_ref.at[d, pl.ds(r, 1)], o_ref.at[pl.ds(row_ref[d * rows + r], 1)], out_sems.at[d, r]
+        )
+
+    for d in range(blocks):
+        take(d).start()
+
+    def send(d, carry):
+        take(d).wait()
+        for r in range(rows):
+            put(d, r).start()
+        return carry
+
+    lax.fori_loop(0, blocks, send, 0)
+
+    def finish(d, carry):
+        for r in range(rows):
+            put(d, r).wait()
+        return carry
+
+    lax.fori_loop(0, blocks, finish, 0)
 
 
 def tables(length, taps):
@@ -243,34 +312,84 @@
 
 def local(raw_traces, filter_index, channel_order, wavelets, damping):
     rows, length = raw_traces.shape
-    taps = wavelets.shape[1]
+    own, taps = wavelets.shape
     n = lax.axis_size("traces")
+    me = lax.axis_index("traces")
     each = rows // n
     floor = damping * (jnp.sum(wavelets * wavelets, axis=1) + 1e-6)
-    packed = jnp.concatenate([wavelets, jnp.broadcast_to(floor[:, None], (floor.shape[0], LANES))], axis=1)
-    bank = lax.all_gather(packed, "traces", axis=0, tiled=True)
-    came = lax.all_to_all(raw_traces.reshape(n, each, length), "traces", 0, 0, tiled=True).reshape(rows, length)
-    picks = lax.all_to_all(filter_index.reshape(n, each), "traces", 0, 0, tiled=True).reshape(rows)
-    chosen = jnp.take(bank, picks, axis=0)
+    picks = filter_index.reshape(own, rows // own).astype(jnp.float32)
+    packed = lax.all_gather(jnp.concatenate([wavelets, floor[:, None], picks], axis=1), "traces", axis=0, tiled=True)
+    all_picks = packed[:, taps + 1 :].reshape(n, n, each).astype(jnp.int32)
+    came_picks = lax.dynamic_index_in_dim(all_picks, me, 1, keepdims=False)
+    bank = jnp.concatenate([packed[:, :taps], jnp.broadcast_to(packed[:, taps : taps + 1], (own * n, LANES))], axis=1)
     fwd, inv, tw = tables(length, taps)
-    whole = lambda a: pl.BlockSpec(a.shape, lambda i: (0,) * a.ndim)
-    result = pl.pallas_call(
-        functools.partial(block_kernel, taps),
-        grid=(rows // ROWS,),
+    whole = lambda a: pl.BlockSpec(a.shape, lambda i, *_: (0,) * a.ndim)
+    fixed = [pl.BlockSpec((ROWS, taps + LANES), lambda i, *_: (i, 0)), whole(fwd), whole(inv), whole(tw)]
+    params = pltpu.CompilerParams(vmem_limit_bytes=48 * 1024 * 1024)
+    places = (jnp.arange(each)[None, :] * n + jnp.arange(n)[:, None]).reshape(-1)
+
+    if each % (2 * SUBLANES):
+        came = lax.all_to_all(raw_traces.reshape(n, each, length), "traces", 0, 0, tiled=True).reshape(rows, length)
+        result = pl.pallas_call(
+            functools.partial(block_kernel, taps, ()),
+            grid=(rows // ROWS,),
+            out_shape=jax.ShapeDtypeStruct((rows, length), jnp.float32),
+            in_specs=[pl.BlockSpec((ROWS, length), lambda i: (i, 0))] + fixed,
+            out_specs=pl.BlockSpec((ROWS, length), lambda i: (i, 0)),
+            scratch_shapes=scratch(),
+            compiler_params=params,
+        )(came, jnp.take(bank, came_picks.reshape(-1), axis=0), fwd, inv, tw)
+        return jnp.take(result, (channel_order % n) * each + channel_order // n, axis=0)
+
+    hits = channel_order[None, :] == places[:, None]
+    row_of = jnp.sum(jnp.where(hits, jnp.arange(rows)[None, :], 0), axis=1).reshape(n, 2, each // 2)
+    part = each // 2
+    group = ROWS // part if part < ROWS else 1
+    split = raw_traces.reshape(n, 2, part, length)
+    steps = n // group
+    flops = pl.CostEstimate(flops=steps * ROWS * length * 1500, bytes_accessed=8 * steps * ROWS * length, transcendentals=0)
+
+    came_raw = lax.all_to_all(split[:, 0], "traces", 0, 0, tiled=True)
+    own_rows = filter_index.reshape(n, 2, part)[:, 1].reshape(-1)
+    done_here = pl.pallas_call(
+        functools.partial(block_kernel, taps, (slice(None), 0)),
+        grid=(steps,),
+        out_shape=jax.ShapeDtypeStruct((n, part, length), jnp.float32),
+        in_specs=[pl.BlockSpec((group, 1, part, length), lambda i: (i, 1, 0, 0))] + fixed,
+        out_specs=pl.BlockSpec((group, part, length), lambda i: (i, 0, 0)),
+        scratch_shapes=scratch(),
+        compiler_params=params,
+        cost_estimate=flops,
+    )(split, jnp.take(bank, own_rows, axis=0), fwd, inv, tw)
+    came_done = lax.all_to_all(done_here, "traces", 0, 0, tiled=True)
+    came_rows = came_picks[:, :part].reshape(-1)
+    filled = pl.pallas_call(
+        functools.partial(place_kernel, taps),
+        grid_spec=pltpu.PrefetchScalarGridSpec(
+            num_scalar_prefetch=1,
+            grid=(steps,),
+            in_specs=[pl.BlockSpec((group, part, length), lambda i, *_: (i, 0, 0))] + fixed,
+            out_specs=pl.BlockSpec(memory_space=pl.ANY),
+            scratch_shapes=scratch()
+            + [pltpu.VMEM((2, ROWS, length), jnp.float32), pltpu.SemaphoreType.DMA((2, ROWS))],
+        ),
         out_shape=jax.ShapeDtypeStruct((rows, length), jnp.float32),
-        in_specs=[
-            pl.BlockSpec((ROWS, length), lambda i: (i, 0)),
-            pl.BlockSpec((ROWS, taps + LANES), lambda i: (i, 0)),
-            whole(fwd),
-            whole(inv),
-            whole(tw),
+        compiler_params=params,
+        cost_estimate=flops,
+    )(row_of[:, 0].reshape(-1), came_raw, jnp.take(bank, came_rows, axis=0), fwd, inv, tw)
+    return pl.pallas_call(
+        settle_kernel,
+        in_specs=[pl.BlockSpec(memory_space=pltpu.SMEM)] + [pl.BlockSpec(memory_space=pl.ANY)] * 2,
+        out_specs=pl.BlockSpec(memory_space=pl.ANY),
+        out_shape=jax.ShapeDtypeStruct((rows, length), jnp.float32),
+        scratch_shapes=[
+            pltpu.VMEM((n, part, length), jnp.float32),
+            pltpu.SemaphoreType.DMA((n,)),
+            pltpu.SemaphoreType.DMA((n, part)),
         ],
-        out_specs=pl.BlockSpec((ROWS, length), lambda i: (i, 0)),
-        scratch_shapes=scratch(),
-        compiler_params=pltpu.CompilerParams(vmem_limit_bytes=40 * 1024 * 1024),
-    )(came, chosen, fwd, inv, tw)
-    source = (channel_order % n) * each + channel_order // n
-    return jnp.take(result, source, axis=0)
+        input_output_aliases={2: 0},
+        compiler_params=params,
+    )(row_of[:, 1].reshape(-1), came_done, filled)
 
 
 def solution(mesh):

time: 273 us -> 238 us (0.87)
  blocking collectives: 203 us -> 102 us
  waiting for transfers between devices: 0.01 us -> 71.7 us
  local copies, waits for them, and re-layouts: 19.1 us -> 9.23 us
  Pallas kernels: 32.9 us -> 41.7 us
  other arithmetic: 8.9 us -> 0.72 us
  starting transfers between devices: 7.33 us -> 11.9 us
    all_gather x1, blocking collectives: 193 us -> 102 us  [local(): lax.all_gather(jnp.concatenate([wavelets, floor[:, None], picks], axis=1)...]
    all_to_all x1 -> x2, waiting for transfers between devices: 0.01 us -> 71.7 us  [the longest x1 71.7 us: local(): came_done = lax.all_to_all(done_here, 'traces', 0, 0, tiled=True)]
    gather x2, local copies, waits for them, and re-layouts: 14.2 us -> 1.53 us  [the longest x1 0.76 us: local(): jnp.take(bank, own_rows, axis=0)]
    all_to_all x1 -> x0, blocking collectives: 10.2 us -> none  [local(): lax.all_to_all(filter_index.reshape(n, each), 'traces', 0, 0, tiled=True)]
    pallas_call x1 -> x3, Pallas kernels: 32.9 us -> 41.7 us  [the longest x1 19.3 us: local(): pl.pallas_call(functools.partial(place_kernel, taps), grid_spec=pltpu.Pre...]
    select_n x3 -> x4, other arithmetic: 8.07 us -> 0.18 us  [the longest x2 0.09 us: local(): jnp.take(bank, came_rows, axis=0)]
    squeeze x0 -> x1, local copies, waits for them, and re-layouts: none -> 4.6 us  [local(): came_raw = lax.all_to_all(split[:, 0], 'traces', 0, 0, tiled=True)]
    all_to_all x1 -> x2, starting transfers between devices: 7.33 us -> 11.9 us  [the longest x1 6.65 us: local(): came_raw = lax.all_to_all(split[:, 0], 'traces', 0, 0, tiled=True)]
  transfers between devices with their start and end apart: 1 -> 2, of which waited for: 0 -> 1; matrix products, arithmetic and copies ran while one was open for 1% -> 1% of each run, Pallas kernels for 0% -> 15%
where the time goes in v2:
time: 238 us
  blocking collectives  102 us (43%)
  waiting for transfers between devices  71.7 us (30%)
  Pallas kernels  41.7 us (18%)
  starting transfers between devices  11.9 us (5%)
  local copies, waits for them, and re-layouts  9.23 us (4%)
    all_gather x1, blocking collectives, local(): lax.all_gather(jnp.concatenate([wavelets, floor[:, None], picks], axis=1)...  102 us
    all_to_all x1, waiting for transfers between devices, local(): came_done = lax.all_to_all(done_here, 'traces', 0, 0, tiled=True)  71.7 us
    pallas_call x1, Pallas kernels, local(): pl.pallas_call(functools.partial(place_kernel, taps), grid_spec=pltpu.Pre...  19.3 us
    pallas_call x1, Pallas kernels, local(): pl.pallas_call(functools.partial(block_kernel, taps, (slice(None), 0)), g...  17 us
    all_to_all x1, starting transfers between devices, local(): came_raw = lax.all_to_all(split[:, 0], 'traces', 0, 0, tiled=True)  6.65 us
    pallas_call x1, Pallas kernels, local(): pl.pallas_call(settle_kernel, in_specs=[pl.BlockSpec(memory_space=pltpu.S...  5.38 us
    all_to_all x1, starting transfers between devices, local(): came_done = lax.all_to_all(done_here, 'traces', 0, 0, tiled=True)  5.2 us
  transfers between devices with their start and end apart: 2, of which 1 were waited for; matrix products, arithmetic and copies ran while one was open for 1% of the time, Pallas kernels for 15%

profile of v2, /device:TPU:13, one launch (start us, length us, event | category | flops | bytes accessed | tf_op | source)
XLA Modules:
  0.0 237.9 jit_solution(176966480410957591)
XLA Ops:
  0.0 4.6 %slice_bitcast_fusion = f32[16,8,8192]{2,1,0:T(8,128)} fusion(f32[16,2,8,8192]{3,2,1,0:T(8,128)} %bitcast.10), kind=kLoop, calls=%fused_computation.2 | loop fusion | bytes 8388608 | tf_op jit(solution)/shard_map/squeeze | solution.py:352
  4.6 0.0 copy-start.5
  4.6 0.0 copy-start.4
  4.6 0.0 copy-start.7
  4.6 6.7 %all-to-all-start.1 = ((f32[16,8,8192]{2,1,0:T(8,128)}), f32[16,8,8192]{2,1,0:T(8,128)}, u32[]{:S(2)}, u32[]{:S(2)}) async-start(f32[16,8,8192]{2,1,0:T(8,128)} %slice_bitcast_fusion), calls=%async_computation.1 | async-start | bytes 8388608 | tf_op jit(solution)/shard_map/all_to_all | solution.py:352
  11.3 0.0 copy-done.5
  11.3 0.0 copy-start.1
  11.3 0.0 copy-start.2
  11.3 0.0 copy-start.3
  11.3 0.1 reshape.43
  11.4 0.1 convert_element_type.13
  11.5 0.0 copy-done.4
  11.5 0.1 multiply_reduce_fusion
  11.6 0.0 copy-done.7
  11.6 0.1 copy.14
  11.8 0.1 reshape_squeeze.10
  11.8 0.1 pad_maximum_fusion.1
  11.9 102.4 %all_gather.3 = f32[256,273]{1,0:T(8,128)S(1)} all-gather(f32[16,273]{1,0:T(8,128)S(1)} %pad_maximum_fusion.1), channel_id=1, replica_groups=mesh['groups'=2,'traces'=16] {'traces'}, dimensions={0}, use_global_device_ids=true | all-gather | bytes 297024 | tf_op jit(solution)/shard_map/all_gather | solution.py:321
  114.4 0.1 slice_reduce_fusion
  114.5 0.1 broadcast_in_dim.39
  114.6 0.8 gather_fusion
  115.4 0.1 broadcast_select_fusion.1.w_ref
  115.5 0.0 copy-done.1
  115.5 0.0 copy-done.2
  115.5 0.0 copy-done.3
  115.5 17.0 %shard_map.82 = f32[16,8,8192]{2,1,0:T(8,128)S(1)} custom-call(f32[16,2,8,8192]{3,2,1,0:T(8,128)} %bitcast.11, f32[128,384]{1,0:T(8,128)S(1)} %broadcast_select_fusion.1.w_ref, bf16[768,256]{1,0:T(8,128)(2,1)S(1)} %copy-done.2, bf16[768,256]{1,0:T(8,128)(2,1)S(1)} %copy-done.1, f32[33,8,128]{2,1,0:T(8,128)S(1)} %copy-done.3), custom_call_target="tpu_custom_call" | custom-call | flops 1572864000 | bytes 8388608 | tf_op jit(solution)/shard_map/pallas_call | solution.py:354
  132.5 0.0 copy-start
  132.6 2.0 copy-done
  134.5 0.0 copy-start.6
  134.5 0.0 all-to-all-done.1.x_ref
  134.5 5.2 %all-to-all-start = ((f32[16,8,8192]{2,1,0:T(8,128)}), f32[16,8,8192]{2,1,0:T(8,128)}, u32[]{:S(2)}, u32[]{:S(2)}) async-start(f32[16,8,8192]{2,1,0:T(8,128)} %copy-done), calls=%async_computation | async-start | bytes 8388608 | tf_op jit(solution)/shard_map/all_to_all | solution.py:364
  139.7 0.1 add.36
  139.8 0.0 copy-done.6
  139.8 0.2 select_reduce_fusion
  140.0 0.1 reshape.41
  140.2 0.1 reshape_squeeze.11.row_ref
  140.3 0.1 reshape_squeeze.9.row_ref
  140.4 0.1 slice_convert_fusion
  140.5 0.1 reshape.44
  140.6 0.8 gather_fusion.1
  141.4 0.1 broadcast_select_fusion.w_ref
  141.5 19.3 %shard_map.83.filled_ref = f32[256,8192]{1,0:T(8,128)} custom-call(s32[128]{0:T(128)S(1)} %reshape_squeeze.11.row_ref, f32[16,8,8192]{2,1,0:T(8,128)} %all-to-all-done.1.x_ref, f32[128,384]{1,0:T(8,128)S(1)} %broadcast_select_fusion.w_ref, bf16[768,256]{1,0:T(8,128)(2,1)S(1)} %copy-done.2, bf16[768,256]{1,0:T(8,128)(2,1)S(1)} %copy-done.1, ...), custom_call_target="tpu_custom_call" | custom-call | flops 1572864000 | bytes 8388608 | tf_op jit(solution)/shard_map/pallas_call | solution.py:366
  160.8 71.7 %all-to-all-done.came_ref = f32[16,8,8192]{2,1,0:T(8,128)} async-done(((f32[16,8,8192]{2,1,0:T(8,128)}), f32[16,8,8192]{2,1,0:T(8,128)}, u32[]{:S(2)}, u32[]{:S(2)}) %all-to-all-start) | async-done | bytes 4194336 | tf_op jit(solution)/shard_map/all_to_all | solution.py:364
  232.5 5.4 %shard_map.84 = f32[256,8192]{1,0:T(8,128)} custom-call(s32[128]{0:T(128)S(1)} %reshape_squeeze.9.row_ref, f32[16,8,8192]{2,1,0:T(8,128)} %all-to-all-done.came_ref, f32[256,8192]{1,0:T(8,128)} %shard_map.83.filled_ref), custom_call_target="tpu_custom_call", output_to_operand_aliasing={{}: (2, {})} | custom-call | tf_op jit(solution)/shard_map/pallas_call | solution.py:380
  (15 shorter events, 0.2 us)
Async XLA Ops:
  4.6 6.7 %copy-start.5 = (s32[256]{0:T(256)S(1)}, s32[256]{0:T(256)}, u32[]{:S(2)}) copy-start(s32[256]{0:T(256)} %param.11) | copy-start | bytes 3076
  4.6 6.9 %copy-start.4 = (f32[16,256]{1,0:T(8,128)S(1)}, f32[16,256]{1,0:T(8,128)}, u32[]{:S(2)}) copy-start(f32[16,256]{1,0:T(8,128)} %param.13) | copy-start | bytes 49156
  4.6 7.0 %copy-start.7 = (f32[16]{0:T(128)S(1)}, f32[16]{0:T(128)}, u32[]{:S(2)}) copy-start(f32[16]{0:T(128)} %param.14) | copy-start | bytes 196
  4.6 129.9 %all-to-all-start.1 = ((f32[16,8,8192]{2,1,0:T(8,128)}), f32[16,8,8192]{2,1,0:T(8,128)}, u32[]{:S(2)}, u32[]{:S(2)}) async-start(f32[16,8,8192]{2,1,0:T(8,128)} %slice_bitcast_fusion), calls=%async_computation.1 | async-start | bytes 8388608 | tf_op jit(solution)/shard_map/all_to_all | solution.py:352
  11.3 104.2 %copy-start.1 = (bf16[768,256]{1,0:T(8,128)(2,1)S(1)}, bf16[768,256]{1,0:T(8,128)(2,1)}, u32[]{:S(2)}) copy-start(bf16[768,256]{1,0:T(8,128)(2,1)} %constant.15.clone.inv_ref) | copy-start | bytes 1179652
  11.3 104.2 %copy-start.2 = (bf16[768,256]{1,0:T(8,128)(2,1)S(1)}, bf16[768,256]{1,0:T(8,128)(2,1)}, u32[]{:S(2)}) copy-start(bf16[768,256]{1,0:T(8,128)(2,1)} %constant.10.clone.fwd_ref) | copy-start | bytes 1179652
  11.3 104.2 %copy-start.3 = (f32[33,8,128]{2,1,0:T(8,128)S(1)}, f32[33,8,128]{2,1,0:T(8,128)}, u32[]{:S(2)}) copy-start(f32[33,8,128]{2,1,0:T(8,128)} %constant.34.clone.tw_ref) | copy-start | bytes 405508
  132.5 2.0 copy-start
  134.5 5.3 %copy-start.6 = (s32[256]{0:T(256)S(1)}, s32[256]{0:T(256)}, u32[]{:S(2)}) copy-start(s32[256]{0:T(256)} %param.12) | copy-start | bytes 3076
  134.5 98.0 %all-to-all-start = ((f32[16,8,8192]{2,1,0:T(8,128)}), f32[16,8,8192]{2,1,0:T(8,128)}, u32[]{:S(2)}, u32[]{:S(2)}) async-start(f32[16,8,8192]{2,1,0:T(8,128)} %copy-done), calls=%async_computation | async-start | bytes 8388608 | tf_op jit(solution)/shard_map/all_to_all | solution.py:364

commit v3 on v2

--- a/solution.py
+++ b/solution.py
@@ -319,6 +319,9 @@
     floor = damping * (jnp.sum(wavelets * wavelets, axis=1) + 1e-6)
     picks = filter_index.reshape(own, rows // own).astype(jnp.float32)
     packed = lax.all_gather(jnp.concatenate([wavelets, floor[:, None], picks], axis=1), "traces", axis=0, tiled=True)
+    part = each // 2
+    first = raw_traces.reshape(n, each, length)[:, :part]
+    first, packed = lax.optimization_barrier((first, packed))
     all_picks = packed[:, taps + 1 :].reshape(n, n, each).astype(jnp.int32)
     came_picks = lax.dynamic_index_in_dim(all_picks, me, 1, keepdims=False)
     bank = jnp.concatenate([packed[:, :taps], jnp.broadcast_to(packed[:, taps : taps + 1], (own * n, LANES))], axis=1)
@@ -343,13 +346,12 @@
 
     hits = channel_order[None, :] == places[:, None]
     row_of = jnp.sum(jnp.where(hits, jnp.arange(rows)[None, :], 0), axis=1).reshape(n, 2, each // 2)
-    part = each // 2
     group = ROWS // part if part < ROWS else 1
     split = raw_traces.reshape(n, 2, part, length)
     steps = n // group
     flops = pl.CostEstimate(flops=steps * ROWS * length * 1500, bytes_accessed=8 * steps * ROWS * length, transcendentals=0)
 
-    came_raw = lax.all_to_all(split[:, 0], "traces", 0, 0, tiled=True)
+    came_raw = lax.all_to_all(first, "traces", 0, 0, tiled=True)
     own_rows = filter_index.reshape(n, 2, part)[:, 1].reshape(-1)
     done_here = pl.pallas_call(
         functools.partial(block_kernel, taps, (slice(None), 0)),

time: 238 us -> 231 us (0.971)
  blocking collectives: 102 us -> 16.7 us
  waiting for transfers between devices: 71.7 us -> 143 us
  starting transfers between devices: 11.9 us -> 15.9 us
  other arithmetic: 0.72 us -> 3.49 us
    all_gather x1, blocking collectives: 102 us -> 16.7 us  [local(): lax.all_gather(jnp.concatenate([wavelets, floor[:, None], picks], axis=1)...]
    all_to_all x1, waiting for transfers between devices: 0.01 us -> 72.1 us  [local(): came_raw = lax.all_to_all(first, 'traces', 0, 0, tiled=True)]
    slice x0 -> x1, local copies, waits for them, and re-layouts: none -> 4.6 us  [local(): first = raw_traces.reshape(n, each, length)[:, :part]]
    squeeze x1 -> x0, local copies, waits for them, and re-layouts: 4.6 us -> none  [local(): came_raw = lax.all_to_all(split[:, 0], 'traces', 0, 0, tiled=True)]
    all_to_all x1, starting transfers between devices: 6.65 us -> 11.1 us  [local(): came_raw = lax.all_to_all(first, 'traces', 0, 0, tiled=True)]
  transfers between devices with their start and end apart: 2 -> 2, of which waited for: 1 -> 2; matrix products, arithmetic and copies ran while one was open for 1% -> 1% of each run, Pallas kernels for 15% -> 16%
where the time goes in v3:
time: 231 us
  waiting for transfers between devices  143 us (62%)
  Pallas kernels  41.7 us (18%)
  blocking collectives  16.7 us (7%)
  starting transfers between devices  15.9 us (7%)
  local copies, waits for them, and re-layouts  9.22 us (4%)
  other arithmetic  3.49 us (2%)
    all_to_all x1, waiting for transfers between devices, local(): came_raw = lax.all_to_all(first, 'traces', 0, 0, tiled=True)  72.1 us
    all_to_all x1, waiting for transfers between devices, local(): came_done = lax.all_to_all(done_here, 'traces', 0, 0, tiled=True)  71.4 us
    pallas_call x1, Pallas kernels, local(): pl.pallas_call(functools.partial(place_kernel, taps), grid_spec=pltpu.Pre...  19.3 us
    pallas_call x1, Pallas kernels, local(): pl.pallas_call(functools.partial(block_kernel, taps, (slice(None), 0)), g...  17 us
    all_gather x1, blocking collectives, local(): lax.all_gather(jnp.concatenate([wavelets, floor[:, None], picks], axis=1)...  16.7 us
    all_to_all x1, starting transfers between devices, local(): came_raw = lax.all_to_all(first, 'traces', 0, 0, tiled=True)  11.1 us
    pallas_call x1, Pallas kernels, local(): pl.pallas_call(settle_kernel, in_specs=[pl.BlockSpec(memory_space=pltpu.S...  5.38 us
    all_to_all x1, starting transfers between devices, local(): came_done = lax.all_to_all(done_here, 'traces', 0, 0, tiled=True)  4.76 us
  transfers between devices with their start and end apart: 2, of which 2 were waited for; matrix products, arithmetic and copies ran while one was open for 1% of the time, Pallas kernels for 16%

profile of v3, /device:TPU:13, one launch (start us, length us, event | category | flops | bytes accessed | tf_op | source)
XLA Modules:
  0.0 230.7 jit_solution(5791961086968669960)
XLA Ops:
  0.0 0.8 multiply_reduce_fusion
  0.8 0.7 convert_element_type.12
  1.5 0.1 convert_element_type.13
  1.6 0.7 multiply_bitcast_fusion
  2.3 0.1 copy.12
  2.3 0.8 pad_maximum_fusion.1
  3.1 16.7 %all_gather.3 = f32[256,273]{1,0:T(8,128)S(1)} all-gather(f32[16,273]{1,0:T(8,128)S(1)} %pad_maximum_fusion.1), channel_id=1, replica_groups=mesh['groups'=2,'traces'=16] {'traces'}, dimensions={0}, use_global_device_ids=true | all-gather | bytes 297024 | tf_op jit(solution)/shard_map/all_gather | solution.py:321
  19.8 4.6 %slice.38 = f32[16,8,8192]{2,1,0:T(8,128)} slice(f32[16,16,8192]{2,1,0:T(8,128)} %bitcast.7), slice={[0:16], [0:8], [0:8192]} | slice | bytes 8388608 | tf_op jit(solution)/shard_map/slice | solution.py:323
  24.4 0.0 copy-start.4
  24.4 0.0 copy-start.1
  24.4 0.0 copy-start.2
  24.4 0.0 copy-start.3
  24.4 11.1 %all-to-all-start.1 = ((f32[16,8,8192]{2,1,0:T(8,128)}), f32[16,8,8192]{2,1,0:T(8,128)}, u32[]{:S(2)}, u32[]{:S(2)}) async-start(f32[16,8,8192]{2,1,0:T(8,128)} %slice.38), calls=%async_computation.1 | async-start | bytes 8388608 | tf_op jit(solution)/shard_map/all_to_all | solution.py:354
  35.6 0.0 copy-done.4
  35.6 0.1 reshape.47
  35.7 0.1 reshape_squeeze.10
  35.8 0.1 slice_reduce_fusion
  36.0 0.1 broadcast_in_dim.39
  36.1 0.8 gather_fusion
  36.9 0.1 broadcast_select_fusion.1.w_ref
  37.0 0.0 copy-done.1
  37.0 0.0 copy-done.2
  37.0 0.0 copy-done.3
  37.0 17.0 %shard_map.82 = f32[16,8,8192]{2,1,0:T(8,128)S(1)} custom-call(f32[16,2,8,8192]{3,2,1,0:T(8,128)} %bitcast.8, f32[128,384]{1,0:T(8,128)S(1)} %broadcast_select_fusion.1.w_ref, bf16[768,256]{1,0:T(8,128)(2,1)S(1)} %copy-done.2, bf16[768,256]{1,0:T(8,128)(2,1)S(1)} %copy-done.1, f32[33,8,128]{2,1,0:T(8,128)S(1)} %copy-done.3), custom_call_target="tpu_custom_call" | custom-call | flops 1572864000 | bytes 8388608 | tf_op jit(solution)/shard_map/pallas_call | solution.py:356
  54.0 0.0 copy-start
  54.0 2.0 copy-done
  56.0 0.0 copy-start.5
  56.0 72.1 %all-to-all-done.1.x_ref = f32[16,8,8192]{2,1,0:T(8,128)} async-done(((f32[16,8,8192]{2,1,0:T(8,128)}), f32[16,8,8192]{2,1,0:T(8,128)}, u32[]{:S(2)}, u32[]{:S(2)}) %all-to-all-start.1) | async-done | bytes 4194336 | tf_op jit(solution)/shard_map/all_to_all | solution.py:354
  128.1 4.8 %all-to-all-start = ((f32[16,8,8192]{2,1,0:T(8,128)}), f32[16,8,8192]{2,1,0:T(8,128)}, u32[]{:S(2)}, u32[]{:S(2)}) async-start(f32[16,8,8192]{2,1,0:T(8,128)} %copy-done), calls=%async_computation | async-start | bytes 8388608 | tf_op jit(solution)/shard_map/all_to_all | solution.py:366
  132.8 0.1 add.36
  132.9 0.0 copy-done.5
  132.9 0.2 select_reduce_fusion
  133.1 0.1 reshape.44
  133.3 0.1 reshape_squeeze.11.row_ref
  133.3 0.1 reshape_squeeze.9.row_ref
  133.4 0.1 slice_convert_fusion
  133.6 0.1 reshape.48
  133.7 0.8 gather_fusion.1
  134.5 0.1 broadcast_select_fusion.w_ref
  134.6 19.3 %shard_map.83.filled_ref = f32[256,8192]{1,0:T(8,128)} custom-call(s32[128]{0:T(128)S(1)} %reshape_squeeze.11.row_ref, f32[16,8,8192]{2,1,0:T(8,128)} %all-to-all-done.1.x_ref, f32[128,384]{1,0:T(8,128)S(1)} %broadcast_select_fusion.w_ref, bf16[768,256]{1,0:T(8,128)(2,1)S(1)} %copy-done.2, bf16[768,256]{1,0:T(8,128)(2,1)S(1)} %copy-done.1, ...), custom_call_target="tpu_custom_call" | custom-call | flops 1572864000 | bytes 8388608 | tf_op jit(solution)/shard_map/pallas_call | solution.py:368
  153.8 71.4 %all-to-all-done.came_ref = f32[16,8,8192]{2,1,0:T(8,128)} async-done(((f32[16,8,8192]{2,1,0:T(8,128)}), f32[16,8,8192]{2,1,0:T(8,128)}, u32[]{:S(2)}, u32[]{:S(2)}) %all-to-all-start) | async-done | bytes 4194336 | tf_op jit(solution)/shard_map/all_to_all | solution.py:366
  225.3 5.4 %shard_map.84 = f32[256,8192]{1,0:T(8,128)} custom-call(s32[128]{0:T(128)S(1)} %reshape_squeeze.9.row_ref, f32[16,8,8192]{2,1,0:T(8,128)} %all-to-all-done.came_ref, f32[256,8192]{1,0:T(8,128)} %shard_map.83.filled_ref), custom_call_target="tpu_custom_call", output_to_operand_aliasing={{}: (2, {})} | custom-call | tf_op jit(solution)/shard_map/pallas_call | solution.py:382
  (13 shorter events, 0.2 us)
Async XLA Ops:
  24.4 11.1 %copy-start.4 = (s32[256]{0:T(256)S(1)}, s32[256]{0:T(256)}, u32[]{:S(2)}) copy-start(s32[256]{0:T(256)} %param.11) | copy-start | bytes 3076
  24.4 12.5 %copy-start.1 = (bf16[768,256]{1,0:T(8,128)(2,1)S(1)}, bf16[768,256]{1,0:T(8,128)(2,1)}, u32[]{:S(2)}) copy-start(bf16[768,256]{1,0:T(8,128)(2,1)} %constant.15.clone.inv_ref) | copy-start | bytes 1179652
  24.4 12.5 %copy-start.2 = (bf16[768,256]{1,0:T(8,128)(2,1)S(1)}, bf16[768,256]{1,0:T(8,128)(2,1)}, u32[]{:S(2)}) copy-start(bf16[768,256]{1,0:T(8,128)(2,1)} %constant.10.clone.fwd_ref) | copy-start | bytes 1179652
  24.4 12.6 %copy-start.3 = (f32[33,8,128]{2,1,0:T(8,128)S(1)}, f32[33,8,128]{2,1,0:T(8,128)}, u32[]{:S(2)}) copy-start(f32[33,8,128]{2,1,0:T(8,128)} %constant.34.clone.tw_ref) | copy-start | bytes 405508
  24.4 103.6 %all-to-all-start.1 = ((f32[16,8,8192]{2,1,0:T(8,128)}), f32[16,8,8192]{2,1,0:T(8,128)}, u32[]{:S(2)}, u32[]{:S(2)}) async-start(f32[16,8,8192]{2,1,0:T(8,128)} %slice.38), calls=%async_computation.1 | async-start | bytes 8388608 | tf_op jit(solution)/shard_map/all_to_all | solution.py:354
  54.0 2.0 copy-start
  56.0 76.9 %copy-start.5 = (s32[256]{0:T(256)S(1)}, s32[256]{0:T(256)}, u32[]{:S(2)}) copy-start(s32[256]{0:T(256)} %param.12) | copy-start | bytes 3076
  128.1 97.2 %all-to-all-start = ((f32[16,8,8192]{2,1,0:T(8,128)}), f32[16,8,8192]{2,1,0:T(8,128)}, u32[]{:S(2)}, u32[]{:S(2)}) async-start(f32[16,8,8192]{2,1,0:T(8,128)} %copy-done), calls=%async_computation | async-start | bytes 8388608 | tf_op jit(solution)/shard_map/all_to_all | solution.py:366
